TPU v7x, 256 devices: a whole 4x4x8 slice. The times are simulated.
256 devices in a mesh: gx: 64 (over x, z, core), gy: 4 (over y).
Axes of the slice: x: 4, y: 4, z: 8, core: 2. Of those that a mesh axis runs over, the one named last changes fastest.
Arguments:
- measures: bfloat16 [2097152, 128], P(('gx', 'gy')), may hold values from -6 to 6
- row_keys: int32 [2097152], P(('gx', 'gy')), may hold values from 0 to 131071, as said below
- orders: bfloat16 [131072, 128], P(('gx', 'gy')), may hold values from -6 to 6
- heavy_keys: int32 [512], replicated, may hold values from 0 to 131071, as said below
- key_slot: int32 [131072], replicated, may hold values from 0 to 131071, as said below
Outputs:
- result: bfloat16 [131072, 128], P(('gx', 'gy'))
- heavy_report: bfloat16 [512, 128], P(('gx', 'gy'))
- slot_rows: float32 [131072], P(('gx', 'gy'))
Inputs may be any that keep to these rules, and one draw needn't show every extreme that they name: `heavy_keys`: for each range block d, entries d * 2 to (d + 1) * 2 - 1 are distinct keys of d * 512 to (d + 1) * 512 - 1. `key_slot`: A permutation. Slot s belongs to owner s // 2048 and to quarter (s // 512) % q with q = 4. Key k lies in range block d = k // 512; every range block has exactly 8 keys with slots of each owner, all in quarter d % q. `row_keys`: in the rows of one device, among rows whose key is not heavy, at most 256 have slots of any one owner and at most 64 distinct keys have slots of any one owner; in every device both bounds are reached by some owner.
All inputs are finite; a program needn't handle non-finite values.
Results may differ from a plain program's by a relative error of at most 0.0021.
Values may be sent and summed in bfloat16 or wider, within the bound.
A program may use at most 64 MiB of HBM per device.

v0:
```python
import functools

import jax
import jax.numpy as jnp
from jax import lax
from jax.experimental import pallas as pl
from jax.experimental.pallas import tpu as pltpu
from jax.sharding import PartitionSpec as P

MESH = pl.DeviceIdType.MESH
LANES = 128
F32 = jnp.float32
BF16 = jnp.bfloat16
I32 = jnp.int32
I16 = jnp.int16
VMEM = pl.BlockSpec(memory_space=pltpu.VMEM)
SMEM = pl.BlockSpec(memory_space=pltpu.SMEM)
LIMIT = 60 * 1024 * 1024
NN = (((1,), (0,)), ((), ()))
NT = (((1,), (1,)), ((), ()))

GX, GY = 64, 4
ROWS = 8192
BLOCK = 2048
CAPK = 64
OWN = 2048
KEY_DEV = 512
KPP = 8
HPD = 2
HPM = HPD * GY
STEPS = 8
CHUNK = STEPS * CAPK
CHUNKS = GX // STEPS
EXTRA = 16
SIDE = 16
MESSAGE = CAPK + SIDE
FULL = 32000.0


def dot(a, b, dims=NN):
    return lax.dot_general(a, b, dims, preferred_element_type=F32)


def iota(shape, dim):
    return lax.broadcasted_iota(I32, shape, dim)


def onehot(mask):
    return jnp.where(mask, 1.0, 0.0).astype(BF16)


def spread16(row):
    wide = jnp.broadcast_to(row, (16, row.shape[1])) - iota((16, row.shape[1]), 0)
    return wide.astype(I16)


def hot16(count, base, value=None):
    one = jnp.ones(base.shape, BF16) if value is None else value
    zero = jnp.zeros(base.shape, BF16)
    tiles = [jnp.where(base == jnp.int16(16 * t), one, zero) for t in range(count // 16)]
    return jnp.concatenate(tiles, axis=0)


def value16(row):
    return jnp.broadcast_to(row, (16, row.shape[1])).astype(BF16)


def pick(wide, mask):
    return jnp.sum(jnp.where(mask, wide, 0.0), axis=0, keepdims=True)


def encode(values):
    largest = jnp.max(jnp.abs(values), axis=1, keepdims=True)
    exponent = jnp.ceil(jnp.log2(jnp.maximum(largest, 1e-30)))
    fixed = jnp.round(values * (jnp.exp2(-exponent) * FULL)).astype(I32)
    eye = iota((LANES, LANES), 0) == iota((LANES, LANES), 1)
    across = [
        jnp.sum(jnp.where(eye, exponent[at : at + LANES], 0.0), axis=0, keepdims=True)
        for at in range(0, values.shape[0], LANES)
    ]
    return fixed, across


def scales_down(across, count, first):
    shape = (count, LANES)
    mask = iota(shape, 1) == iota(shape, 0) + first
    column = jnp.sum(jnp.where(mask, across, 0.0), axis=1, keepdims=True)
    return jnp.exp2(column) * (1.0 / FULL)


def prepare(keys, heavy, key_slot, seg_out, heavy_out, meta_out, slots, hist, meta):
    me = lax.axis_index("gx")
    hk = heavy[...]
    order = iota((1, hk.shape[1]), 1) & 1
    low = hot16(256, spread16(hk & 255), value16((order + 1).astype(F32)))
    flags = dot(low, hot16(512, spread16(hk >> 8)), NT)
    even = key_slot[pl.ds(0, 512, stride=2), :]
    odd = key_slot[pl.ds(1, 512, stride=2), :]

    def turned(part):
        return jnp.concatenate([part(even).astype(F32).T, part(odd).astype(F32).T], axis=0)

    first = jnp.where(flags > 0.0, -flags, turned(lambda s: s & 255))
    second = turned(lambda s: (s >> 8) - 256)
    table = jnp.concatenate([first, second], axis=0).astype(BF16)
    hist[...] = jnp.zeros(hist.shape, F32)
    low_index = iota((256, BLOCK), 0)

    @pl.loop(0, ROWS // BLOCK)
    def _(b):
        span = pl.ds(pl.multiple_of(b * BLOCK, BLOCK), BLOCK)
        key = keys[:, span]
        wide = dot(table, hot16(512, spread16(key >> 8)))
        mask = low_index == (key & 255)
        part = pick(wide[:256], mask).astype(I32)
        slot = (pick(wide[256:], mask).astype(I32) + 256) * 256 + part
        is_heavy = part < 0
        slot = jnp.where(is_heavy, -1, slot)
        slots[:, span] = slot
        spot = (((key >> 9) * HPD - 1 - part) - me * HPM) & (GX * HPM - 1)
        heavy_out[:, span] = jnp.where(is_heavy, spot, -1)
        hist[...] += dot(hot16(512, spread16(slot >> 8)), hot16(256, spread16(slot & 255)), NT)

    present = hist[...] > 0.0
    flag = onehot(present)
    inside = dot(flag, onehot(iota((256, 256), 0) < iota((256, 256), 1)))
    whole = dot(flag, jnp.ones((256, LANES), BF16))
    row, col = iota((512, 512), 0), iota((512, 512), 1)
    before = dot(onehot((col < row) & (col >> 3 == row >> 3)), whole.astype(BF16))
    rank = inside + jnp.concatenate([before, before], axis=1)
    ranks = jnp.where(present, rank, 0.0).T.astype(BF16)
    meta[...] = jnp.zeros(meta.shape, F32)

    @pl.loop(0, ROWS // BLOCK)
    def _(b):
        span = pl.ds(pl.multiple_of(b * BLOCK, BLOCK), BLOCK)
        slot = slots[:, span]
        heavy_spot = heavy_out[:, span]
        light = slot >= 0
        wide = dot(ranks, hot16(512, spread16(slot >> 8)))
        place = pick(wide, low_index == (slot & 255)).astype(I32)
        seg = (((slot >> 11) - me) & (GX - 1)) * CAPK + place
        seg = jnp.where(light, seg, -1)
        seg_out[:, span] = seg
        base = spread16(jnp.where(light, place, -1))
        kinds = jnp.concatenate(
            [
                hot16(64, base),
                hot16(64, base, value16((slot & 255).astype(F32))),
                hot16(64, base, value16(((slot >> 8) & 7).astype(F32))),
                hot16(64, spread16(jnp.where(light, -1, heavy_spot & (HPM - 1)))),
            ],
            axis=0,
        )
        step = jnp.where(light, seg >> 6, heavy_spot >> 3)
        meta[...] += dot(kinds, hot16(LANES, spread16(step)), NT)

    turn = meta[...].T
    left = iota((GX, LANES), 1) < 64

    def doubled(pair):
        swapped = pltpu.roll(pair, 64, 1)
        return jnp.where(left, pair, swapped), jnp.where(left, swapped, pair)

    count, low_sum = doubled(turn[:GX, :LANES])
    high_sum, heavies = doubled(turn[:GX, LANES:])
    share = 1.0 / jnp.maximum(count, 1.0)
    low_slot = jnp.floor(low_sum * share + 0.5)
    high_slot = jnp.floor(high_sum * share + 0.5)
    slot = jnp.where(count > 0.0, high_slot * 256.0 + low_slot, -1.0)
    blank = jnp.zeros((GX, LANES), F32)
    for k, rows in enumerate([count, slot, heavies] + [blank] * 5):
        meta_out[:, k, :] = rows.astype(I32)


def owner_table(me, key_slot, local, rank, spread, sp):
    mine_slot = key_slot[...] - me * OWN
    mine = (mine_slot >= 0) & (mine_slot < OWN)
    flag = onehot(mine)
    inside = dot(flag, onehot(iota((LANES, LANES), 0) < iota((LANES, LANES), 1)))
    whole = dot(flag, jnp.ones((LANES, LANES), BF16))
    line = iota(whole.shape, 0) & 3
    for t in range(1, 4):
        inside = inside + jnp.where(line >= t, pltpu.roll(whole, t, 0), 0.0)
    rank[...] = jnp.where(mine, inside, -1.0)
    local[...] = mine_slot.astype(F32)
    eight = iota((KPP, LANES), 0).astype(F32)

    @pl.loop(0, GX)
    def _(x):
        at = pl.ds(pl.multiple_of(x * 16, 16), 16)
        ranks, locals_ = rank[at, :], local[at, :]
        for y in range(GY):
            acc = jnp.zeros((KPP, LANES), F32)
            for j in range(4):
                n = y * 4 + j
                acc = acc + jnp.where(eight == ranks[n : n + 1], locals_[n : n + 1], 0.0)
            spread[pl.ds(pl.multiple_of(y * KEY_DEV + x * KPP, KPP), KPP), :] = acc

    slot = jnp.sum(spread[...], axis=1, keepdims=True)
    sp[...] = jnp.broadcast_to(slot, spread.shape).astype(I32).astype(I16)


def join_table(me_x, me_y, key_slot, perm):
    first = (me_x * GY + me_y) * 4
    owner = (key_slot[pl.ds(first, 4), :] >> 11).astype(F32)
    across = jnp.concatenate([owner[j : j + 1] for j in range(4)], axis=1)
    down = jnp.concatenate([owner, owner], axis=0).T
    index = iota((LANES, KEY_DEV), 1)
    for j in range(4):
        column = down[:, j : j + 1]
        earlier = index < iota((LANES, KEY_DEV), 0) + j * LANES
        same = jnp.where((column == across) & earlier, 1.0, 0.0)
        rank = jnp.sum(same, axis=1, keepdims=True).astype(I32)
        step = (me_x - column.astype(I32)) & (GX - 1)
        perm[j * LANES : (j + 1) * LANES, :] = onehot(step * KPP + rank == index)


def fused(
    heavy, seg, heavy_seg, meta, measures, key_slot, orders,
    result, report, slot_rows,
    send, got, side, acc, sp, spread, local, rank, perm,
    out2, in2, out3, in3, totals, hist, heavies, tallies,
    s_main, r_main, s_two, r_two, s_three, r_three,
):
    me_x, me_y = lax.axis_index("gx"), lax.axis_index("gy")
    barrier = pltpu.get_barrier_semaphore()

    def along_x(s):
        return (lax.rem(me_x + s, GX), me_y)

    def along_y(s):
        return (me_x, lax.rem(me_y + s, GY))

    def copy(src, dst, send_sem, recv_sem, s, target):
        return pltpu.make_async_remote_copy(
            src_ref=src, dst_ref=dst, send_sem=send_sem.at[s], recv_sem=recv_sem.at[s],
            device_id=target, device_id_type=MESH,
        )

    def main_copy(s):
        return copy(send.at[s], got.at[s], s_main, r_main, s, along_x(s))

    def two_copy(s):
        return copy(out2.at[s], in2.at[s], s_two, r_two, s, along_y(s))

    def three_copy(s):
        x = lax.rem(me_x + s, GX)
        return copy(out3.at[x], in3.at[s], s_three, r_three, s, (x, me_y))

    @pl.loop(1, GX)
    def _(s):
        pl.semaphore_signal(barrier, inc=1, device_id=along_x(s), device_id_type=MESH)

    for s in range(1, GY):
        pl.semaphore_signal(barrier, inc=1, device_id=along_y(s), device_id_type=MESH)

    def segment_sums(row, base):
        total = jnp.zeros((CHUNK, LANES), F32)
        for b in range(ROWS // BLOCK):
            span = slice(b * BLOCK, (b + 1) * BLOCK)
            hot = hot16(CHUNK, spread16(row[:, span] - base))
            total = total + dot(hot, measures[span, :])
        return total

    fixed, exponents = encode(segment_sums(heavy_seg, 0))
    last = iota((8, LANES), 0) == 7
    for s in range(GX):
        side[s, 0:HPM] = fixed[s * HPM : (s + 1) * HPM]
        side[s, HPM:SIDE] = jnp.where(last, exponents[s // 16].astype(I32), meta[s])

    left = iota((1, LANES), 1) < CAPK
    scale_line = iota((SIDE, LANES), 0) == SIDE - 2
    pl.semaphore_wait(barrier, GX - 1 + GY - 1)

    @pl.loop(0, CHUNKS)
    def _(c):
        fixed, exponents = encode(segment_sums(seg, c * CHUNK))
        for i in range(STEPS):
            s = c * STEPS + i
            pair = exponents[i // 2].astype(I32)
            swapped = pltpu.roll(pair, CAPK, 1)
            both = jnp.where(left, swapped, pair) if i % 2 else jnp.where(left, pair, swapped)
            send[s, 0:CAPK] = fixed[i * CAPK : (i + 1) * CAPK].astype(I16)
            send[s, CAPK:MESSAGE] = jnp.where(scale_line, both, side[s]).astype(I16)

        @pl.when(c == 0)
        def _():
            got[0] = send[0]

        @pl.when(c > 0)
        def _():
            @pl.loop(jnp.maximum((c - 1) * STEPS, 1), c * STEPS)
            def _(s):
                main_copy(s).start()

    owner_table(me_x, key_slot, local, rank, spread, sp)

    @pl.loop((CHUNKS - 1) * STEPS, GX)
    def _(s):
        main_copy(s).start()

    join_table(me_x, me_y, key_slot, perm)
    acc[...] = jnp.zeros(acc.shape, F32)
    hist[...] = jnp.zeros(hist.shape, F32)
    heavies[...] = jnp.zeros(heavies.shape, F32)
    tallies[...] = jnp.zeros(tallies.shape, F32)

    @pl.loop(0, CHUNKS)
    def _(g):
        @pl.loop(jnp.maximum(g * STEPS, 1), (g + 1) * STEPS)
        def _(s):
            main_copy(s).wait_recv()

        hots, slots, counts = [], [], []
        heavy_sum, heavy_tally = heavies[...], tallies[0:1, :]
        for j in range(STEPS // 2):
            blocks = []
            for i in range(2):
                s = g * STEPS + 2 * j + i
                block = got[s, CAPK:MESSAGE].astype(I32)
                exponents = block[SIDE - 1 : SIDE].astype(F32)
                scale = scales_down(exponents, HPM, (s & 15) * HPM)
                heavy_sum = heavy_sum + block[:HPM].astype(F32) * scale
                heavy_tally = heavy_tally + block[HPM + 2 : HPM + 3].astype(F32)
                blocks.append(block[HPM:])
            rows = jnp.where(left, blocks[0], blocks[1])
            slot = rows[1:2]
            slots.append(slot)
            counts.append(rows[0:1].astype(F32))
            target = jnp.broadcast_to(slot, (16, LANES)).astype(I16)
            one = value16(jnp.exp2(rows[6:7].astype(F32)))
            zero = jnp.zeros((16, LANES), BF16)
            hots.append(
                jnp.concatenate(
                    [
                        jnp.where(sp[16 * t : 16 * t + 16, :] == target, one, zero)
                        for t in range(OWN // 16)
                    ],
                    axis=0,
                )
            )
        heavies[...] = heavy_sum
        tallies[0:1, :] = heavy_tally
        rows = got[pl.ds(g * STEPS, STEPS), 0:CAPK].reshape(CHUNK, LANES).astype(I32)
        pieces = [(rows >> 8).astype(F32).astype(BF16), (rows & 255).astype(F32).astype(BF16)]
        found = dot(jnp.concatenate(hots, axis=1), jnp.concatenate(pieces, axis=1))
        acc[...] += found[:, :LANES] * (256.0 / FULL) + found[:, LANES:] * (1.0 / FULL)
        slot = jnp.concatenate(slots, axis=1)
        count = value16(jnp.concatenate(counts, axis=1))
        hist[...] += dot(
            hot16(16, spread16(slot >> 7)), hot16(LANES, spread16(slot & 127), count), NT
        )

    tally = tallies[0:1, :]
    tally_high = jnp.floor(tally * (1.0 / 16384.0))
    tally_low = tally - tally_high * 16384.0
    heavy_fixed, heavy_exponents = encode(
        jnp.concatenate([heavies[...], jnp.zeros((LANES - HPM, LANES), F32)], axis=0)
    )
    spread[0:HPM, :] = heavy_fixed[:HPM].astype(F32)
    for s in range(1, GY):
        q = lax.rem(me_y + s, GY)
        fixed, exponents = encode(acc[pl.ds(pl.multiple_of(q * KEY_DEV, KEY_DEV), KEY_DEV), :])
        extra = jnp.concatenate(
            [
                hist[pl.ds(q * 4, 4), :],
                *exponents,
                spread[pl.ds(q * HPD, HPD), :],
                heavy_exponents[0], tally_low, tally_high,
                jnp.zeros((3, LANES), F32),
            ],
            axis=0,
        )
        out2[s, KEY_DEV : KEY_DEV + EXTRA] = extra.astype(I32).astype(I16)
        out2[s, 0:KEY_DEV] = fixed.astype(I16)
        if s > 1:
            two_copy(s - 1).start()
    mine = acc[pl.ds(pl.multiple_of(me_y * KEY_DEV, KEY_DEV), KEY_DEV), :]
    slot = sp[pl.ds(pl.multiple_of(me_y * KEY_DEV, KEY_DEV), KEY_DEV), :].astype(I32)
    slot = slot - me_y * KEY_DEV
    totals[...] = mine
    two_copy(GY - 1).start()

    @pl.loop(1, GX)
    def _(s):
        main_copy(s).wait_send()

    slot_total = hist[pl.ds(me_y * 4, 4), :]
    heavy_total = heavies[pl.ds(me_y * HPD, HPD), :]
    for s in range(1, GY):
        two_copy(s).wait_recv()
        part = in2[s, KEY_DEV : KEY_DEV + EXTRA].astype(I32).astype(F32)
        slot_total = slot_total + part[0:4]
        heavy_total = heavy_total + part[8:10] * scales_down(part[10:11], HPD, me_y * HPD)
        tally = tally + part[11:12] + 16384.0 * part[12:13]
        for j in range(4):
            at = slice(j * LANES, (j + 1) * LANES)
            scale = scales_down(part[4 + j : 5 + j], LANES, 0)
            totals[at, :] += in2[s, at].astype(I32).astype(F32) * scale
    slot_rows[...] = slot_total
    wide = jnp.zeros((KEY_DEV, LANES), F32)
    for r in range(4):
        wide = wide + jnp.where(slot >> 7 == r, slot_total[r : r + 1], 0.0)
    wide = jnp.where((slot & 127) == iota((KEY_DEV, LANES), 1), wide, 0.0)
    count = jnp.sum(wide, axis=1, keepdims=True)
    totals[...] = totals[...] * lax.rsqrt(1.0 + count)
    for x in range(GX):
        out3[x] = totals[x * KPP : (x + 1) * KPP, :]
    device = me_x * GY + me_y
    lane = iota((1, LANES), 1)
    sized = []
    for h in range(HPD):
        number = jnp.sum(jnp.where(lane == me_y * HPD + h, tally, 0.0), axis=1, keepdims=True)
        sized.append(heavy_total[h : h + 1] * lax.rsqrt(1.0 + number))
    in3[0] = totals[pl.ds(pl.multiple_of(me_x * KPP, KPP), KPP), :]

    @pl.loop(1, GX)
    def _(s):
        three_copy(s).start()

    line = iota((KEY_DEV, LANES), 0)
    attributes = orders[...].astype(F32)
    heavy_part = jnp.zeros((KEY_DEV, LANES), F32)
    lines = []
    for h in range(HPD):
        spot = heavy[device * HPD + h] - device * KEY_DEV
        here = line == spot
        heavy_part = heavy_part + jnp.where(here, sized[h], 0.0)
        lines.append(jnp.sum(jnp.where(here, attributes, 0.0), axis=0, keepdims=True) * sized[h])
    report[...] = jnp.concatenate(lines, axis=0).astype(BF16)
    for s in range(1, GY):
        two_copy(s).wait_send()

    @pl.loop(1, GX)
    def _(s):
        three_copy(s).wait_recv()

    rows = in3[...].reshape(KEY_DEV, LANES)
    high = rows.astype(BF16)
    low = (rows - high.astype(F32)).astype(BF16)
    both = dot(perm[...], jnp.concatenate([high, low], axis=1))
    found = both[:, :LANES] + both[:, LANES:] + heavy_part
    result[...] = (attributes * found).astype(BF16)

    @pl.loop(1, GX)
    def _(s):
        three_copy(s).wait_send()


def shaped(*dims, dtype=F32):
    return jax.ShapeDtypeStruct(dims, dtype)


def body(measures, row_keys, orders, heavy_keys, key_slot):
    table = key_slot.reshape(key_slot.shape[0] // LANES, LANES)
    seg, heavy_seg, meta = pl.pallas_call(
        prepare,
        out_shape=(
            shaped(1, ROWS, dtype=I32),
            shaped(1, ROWS, dtype=I32),
            shaped(GX, 8, LANES, dtype=I32),
        ),
        in_specs=[VMEM] * 3,
        out_specs=(VMEM,) * 3,
        scratch_shapes=[
            pltpu.VMEM((1, ROWS), I32),
            pltpu.VMEM((512, 256), F32),
            pltpu.VMEM((256, LANES), F32),
        ],
        compiler_params=pltpu.CompilerParams(vmem_limit_bytes=LIMIT),
    )(row_keys.reshape(1, ROWS), heavy_keys.reshape(1, -1), table)
    dma = pltpu.SemaphoreType.DMA
    result, report, slot_rows = pl.pallas_call(
        fused,
        out_shape=(
            shaped(KEY_DEV, LANES, dtype=BF16),
            shaped(HPD, LANES, dtype=BF16),
            shaped(KEY_DEV // LANES, LANES),
        ),
        in_specs=[SMEM] + [VMEM] * 6,
        out_specs=(VMEM,) * 3,
        scratch_shapes=[
            pltpu.VMEM((GX, MESSAGE, LANES), I16),
            pltpu.VMEM((GX, MESSAGE, LANES), I16),
            pltpu.VMEM((GX, SIDE, LANES), I32),
            pltpu.VMEM((OWN, LANES), F32),
            pltpu.VMEM((OWN, LANES), I16),
            pltpu.VMEM((OWN, LANES), F32),
            pltpu.VMEM((1024, LANES), F32),
            pltpu.VMEM((1024, LANES), F32),
            pltpu.VMEM((KEY_DEV, KEY_DEV), BF16),
            pltpu.VMEM((GY, KEY_DEV + EXTRA, LANES), I16),
            pltpu.VMEM((GY, KEY_DEV + EXTRA, LANES), I16),
            pltpu.VMEM((GX, KPP, LANES), F32),
            pltpu.VMEM((GX, KPP, LANES), F32),
            pltpu.VMEM((KEY_DEV, LANES), F32),
            pltpu.VMEM((16, LANES), F32),
            pltpu.VMEM((HPM, LANES), F32),
            pltpu.VMEM((8, LANES), F32),
        ]
        + [dma((GX,))] * 2
        + [dma((GY,))] * 2
        + [dma((GX,))] * 2,
        compiler_params=pltpu.CompilerParams(
            collective_id=0, has_side_effects=True, vmem_limit_bytes=LIMIT
        ),
    )(heavy_keys, seg, heavy_seg, meta, measures, table, orders)
    return (result, report, slot_rows.reshape(KEY_DEV))


def solution(mesh):
    return jax.shard_map(
        body,
        mesh=mesh,
        in_specs=(P(("gx", "gy"), None), P(("gx", "gy")), P(("gx", "gy"), None), P(), P()),
        out_specs=(P(("gx", "gy"), None), P(("gx", "gy"), None), P(("gx", "gy"))),
        check_vma=False,
    )
```

profile of v0, /device:TPU:1, one launch (start us, length us, event | category | flops | bytes accessed | tf_op | source)
XLA Modules:
  0.0 94.4 jit_solution(6928173687552877229)
XLA Ops:
  0.6 16.3 %shard_map.76 = (s32[1,8192]{1,0:T(1,128)}, s32[1,8192]{1,0:T(1,128)}, s32[64,8,128]{2,1,0:T(8,128)}) custom-call(s32[1,8192]{1,0:T(1,128)} %bitcast.6, s32[1,512]{1,0:T(1,128)} %bitcast.7, s32[1024,128]{1,0:T(8,128)} %bitcast.4), custom_call_target="tpu_custom_call" | custom-call | tf_op jit(solution)/shard_map/pallas_call | solution.py:457
  17.0 73.4 %shard_map.77 = (bf16[512,128]{1,0:T(8,128)(2,1)}, bf16[2,128]{1,0:T(2,128)(2,1)}, f32[4,128]{1,0:T(4,128)}) custom-call(s32[512]{0:T(512)} %heavy.1, s32[1,8192]{1,0:T(1,128)} %get-tuple-element.9.seg, s32[1,8192]{1,0:T(1,128)} %get-tuple-element.10.heavy_seg, s32[64,8,128]{2,1,0:T(8,128)} %get-tuple-element.11.meta, bf16[8192,128]{1,0:T(8,128)(2,1)} %measures.1, ...), custom_call_target="tpu_custom_call" | custom-call | tf_op jit(solution)/shard_map/pallas_call | solution.py:474
  90.4 1.6 %copy.11 = bf16[512,128]{1,0:T(8,128)(2,1)} copy(bf16[512,128]{1,0:T(8,128)(2,1)} %get-tuple-element.18) | data formatting | bytes 262144
  92.0 1.2 %copy.12 = bf16[2,128]{1,0:T(2,128)(2,1)} copy(bf16[2,128]{1,0:T(2,128)(2,1)} %get-tuple-element.19) | data formatting | bytes 1024
  93.1 1.3 %copy.13 = f32[512]{0:T(512)} copy(f32[512]{0:T(512)} %bitcast.8) | data formatting | bytes 4096
where the time goes:
time: 94.6 us; the launch traced here: 94.4 us
  Pallas kernels  89.7 us (95%)
  local copies, waits for them, and re-layouts  4.01 us (4%)
    pallas_call x1, Pallas kernels, body(): pl.pallas_call(fused, out_shape=(shaped(KEY_DEV, LANES, dtype=BF16), shap...  73.4 us
    pallas_call x1, Pallas kernels, body(): pl.pallas_call(prepare, out_shape=(shaped(1, ROWS, dtype=I32), shaped(1,...  16.3 us
    unnamed x3, local copies, waits for them, and re-layouts  4.01 us

commit v1 on v0

v1 whole, which is shorter than its diff:
```python
import functools

import jax
import jax.numpy as jnp
from jax import lax
from jax.experimental import pallas as pl
from jax.experimental.pallas import tpu as pltpu
from jax.sharding import PartitionSpec as P

MESH = pl.DeviceIdType.MESH
LANES = 128
F32 = jnp.float32
BF16 = jnp.bfloat16
I32 = jnp.int32
I16 = jnp.int16
VMEM = pl.BlockSpec(memory_space=pltpu.VMEM)
SMEM = pl.BlockSpec(memory_space=pltpu.SMEM)
ANY = pl.BlockSpec(memory_space=pl.ANY)
LIMIT = 60 * 1024 * 1024
NN = (((1,), (0,)), ((), ()))
NT = (((1,), (1,)), ((), ()))

GX, GY = 64, 4
MEMBERS, GROUPS = 64, 4
ROWS = 8192
BLOCK = 2048
CAPK = 64
OWN = 2048
OWN_ROWS = OWN // 128
KEY_DEV = 512
KPP = 8
HPD = 2
HPG = HPD * MEMBERS
STEPS = 8
HALF = CAPK // 2
CHUNK = STEPS * HALF
CHUNKS = MEMBERS // STEPS
EXTRA = 32
FULL = 32000.0


def dot(a, b, dims=NN):
    return lax.dot_general(a, b, dims, preferred_element_type=F32)


def iota(shape, dim):
    return lax.broadcasted_iota(I32, shape, dim)


def onehot(mask):
    return jnp.where(mask, 1.0, 0.0).astype(BF16)


def spread16(row):
    wide = jnp.broadcast_to(row, (16, row.shape[1])) - iota((16, row.shape[1]), 0)
    return wide.astype(I16)


def hot16(count, base, value=None):
    one = jnp.ones(base.shape, BF16) if value is None else value
    zero = jnp.zeros(base.shape, BF16)
    tiles = [jnp.where(base == jnp.int16(16 * t), one, zero) for t in range(count // 16)]
    return jnp.concatenate(tiles, axis=0)


def value16(row):
    return jnp.broadcast_to(row, (16, row.shape[1])).astype(BF16)


def pick(wide, mask):
    return jnp.sum(jnp.where(mask, wide, 0.0), axis=0, keepdims=True)


def power_of(values):
    largest = jnp.max(jnp.abs(values), axis=1, keepdims=True)
    exponent = jnp.ceil(jnp.log2(jnp.maximum(largest, 1e-30)))
    return jnp.round(values * (jnp.exp2(-exponent) * FULL)).astype(I32), exponent


def encode(values):
    fixed, exponent = power_of(values)
    eye = iota((LANES, LANES), 0) == iota((LANES, LANES), 1)
    across = [
        jnp.sum(jnp.where(eye, exponent[at : at + LANES], 0.0), axis=0, keepdims=True)
        for at in range(0, values.shape[0], LANES)
    ]
    return fixed, across


def scales_down(across, count, first):
    shape = (count, LANES)
    mask = iota(shape, 1) == iota(shape, 0) + first
    column = jnp.sum(jnp.where(mask, across, 0.0), axis=1, keepdims=True)
    return jnp.exp2(column) * (1.0 / FULL)


def member_of(block):
    member = (block >> 6) * 16 + (block & 3) * 4 + ((block >> 3) & 1) * 2 + ((block >> 2) & 1)
    return member, (block >> 4) & 3


def find_slots(keys, heavy, key_slot, slots, heavy_spot, hist, heavy_hist):
    hk = heavy[...]
    order = iota((1, hk.shape[1]), 1) & 1
    low = hot16(256, spread16(hk & 255), value16((order + 1).astype(F32)))
    flags = dot(low, hot16(512, spread16(hk >> 8)), NT)
    even = key_slot[pl.ds(0, 512, stride=2), :]
    odd = key_slot[pl.ds(1, 512, stride=2), :]

    def turned(part):
        return jnp.concatenate([part(even).astype(F32).T, part(odd).astype(F32).T], axis=0)

    first = jnp.where(flags > 0.0, -flags, turned(lambda s: s & 255))
    second = turned(lambda s: (s >> 8) - 256)
    table = jnp.concatenate([first, second], axis=0).astype(BF16)
    hist[...] = jnp.zeros(hist.shape, F32)
    heavy_hist[...] = jnp.zeros(heavy_hist.shape, F32)
    low_index = iota((256, BLOCK), 0)

    @pl.loop(0, ROWS // BLOCK)
    def _(b):
        span = pl.ds(pl.multiple_of(b * BLOCK, BLOCK), BLOCK)
        key = keys[:, span]
        wide = dot(table, hot16(512, spread16(key >> 8)))
        mask = low_index == (key & 255)
        part = pick(wide[:256], mask).astype(I32)
        slot = (pick(wide[256:], mask).astype(I32) + 256) * 256 + part
        is_heavy = part < 0
        slot = jnp.where(is_heavy, -1, slot)
        slots[:, span] = slot
        member, group = member_of(key >> 9)
        spot = jnp.where(is_heavy, group * HPG + member * HPD - 1 - part, -1)
        heavy_spot[:, span] = spot
        hist[...] += dot(hot16(512, spread16(slot >> 8)), hot16(256, spread16(slot & 255)), NT)
        heavy_hist[...] += dot(
            hot16(16, spread16(spot >> 7)), hot16(LANES, spread16(spot & 127)), NT
        )


def find_ranks(me, slots, heavy_spot, seg_out, hist, meta, side, measures, pairs):
    present = hist[...] > 0.0
    flag = onehot(present)
    inside = dot(flag, onehot(iota((256, 256), 0) < iota((256, 256), 1)))
    whole = dot(flag, jnp.ones((256, LANES), BF16))
    row, col = iota((512, 512), 0), iota((512, 512), 1)
    before = dot(onehot((col < row) & (col >> 3 == row >> 3)), whole.astype(BF16))
    rank = inside + jnp.concatenate([before, before], axis=1)
    ranks = jnp.where(present, rank, 0.0).T.astype(BF16)
    meta[...] = jnp.zeros(meta.shape, F32)
    low_index = iota((256, BLOCK), 0)

    @pl.loop(0, ROWS // BLOCK)
    def _(b):
        span = pl.ds(pl.multiple_of(b * BLOCK, BLOCK), BLOCK)
        slot = slots[:, span]
        light = slot >= 0
        wide = dot(ranks, hot16(512, spread16(slot >> 8)))
        place = pick(wide, low_index == (slot & 255)).astype(I32)
        step = ((slot >> 11) - me) & (MEMBERS - 1)
        seg_out[:, span] = jnp.where(light, step * HALF + (place & (HALF - 1)), -1)
        bit = jnp.where(light, place >> 5, heavy_spot[:, span] & 1).astype(F32)
        bits = [bit[:, i * LANES : (i + 1) * LANES] for i in range(BLOCK // LANES)]
        down = jnp.concatenate(bits, axis=0).T
        for i in range(BLOCK // LANES):
            at = pl.ds(pl.multiple_of(b * BLOCK + i * LANES, LANES), LANES)
            rows = measures[at, :]
            upper = rows * jnp.broadcast_to(down[:, i : i + 1], (LANES, LANES)).astype(BF16)
            pairs[at, LANES:] = upper
            pairs[at, :LANES] = rows - upper
        base = spread16(jnp.where(light, place, -1))
        kinds = jnp.concatenate(
            [
                hot16(64, base),
                hot16(64, base, value16((slot & 255).astype(F32))),
                hot16(64, base, value16(((slot >> 8) & 7).astype(F32))),
            ],
            axis=0,
        )
        meta[0:192, :] += dot(kinds, hot16(LANES, spread16(jnp.where(light, step, -1))), NT)

    turn = meta[...].T
    left = iota((MEMBERS, LANES), 1) < CAPK

    def doubled(pair):
        swapped = pltpu.roll(pair, CAPK, 1)
        return jnp.where(left, pair, swapped), jnp.where(left, swapped, pair)

    count, low_sum = doubled(turn[:MEMBERS, :LANES])
    high_sum, unused = doubled(turn[:MEMBERS, LANES:])
    share = 1.0 / jnp.maximum(count, 1.0)
    low_slot = jnp.floor(low_sum * share + 0.5)
    high_slot = jnp.floor(high_sum * share + 0.5)
    slot = jnp.where(count > 0.0, high_slot * 256.0 + low_slot, -1.0)
    side[:, 0, :] = count
    side[:, 1, :] = slot
    side[:, 3, :] = jnp.zeros((MEMBERS, LANES), F32)


def owner_table(me, key_slot, local, rank, spread, sp):
    mine_slot = key_slot[...] - me * OWN
    mine = (mine_slot >= 0) & (mine_slot < OWN)
    flag = onehot(mine)
    inside = dot(flag, onehot(iota((LANES, LANES), 0) < iota((LANES, LANES), 1)))
    whole = dot(flag, jnp.ones((LANES, LANES), BF16))
    line = iota(whole.shape, 0) & 3
    for t in range(1, 4):
        inside = inside + jnp.where(line >= t, pltpu.roll(whole, t, 0), 0.0)
    rank[...] = jnp.where(mine, inside, -1.0)
    local[...] = mine_slot.astype(F32)
    eight = iota((KPP, LANES), 0).astype(F32)

    @pl.loop(0, GX)
    def _(x):
        at = pl.ds(pl.multiple_of(x * 16, 16), 16)
        ranks, locals_ = rank[at, :], local[at, :]
        for y in range(GY):
            acc = jnp.zeros((KPP, LANES), F32)
            for j in range(4):
                n = y * 4 + j
                acc = acc + jnp.where(eight == ranks[n : n + 1], locals_[n : n + 1], 0.0)
            first = ((x >> 2) & 3) * KEY_DEV
            first = first + ((x >> 4) * 16 + y * 4 + ((x >> 1) & 1) * 2 + (x & 1)) * KPP
            spread[pl.ds(pl.multiple_of(first, KPP), KPP), :] = acc

    slot = jnp.sum(spread[...], axis=1, keepdims=True)
    sp[...] = jnp.broadcast_to(slot, spread.shape).astype(I32).astype(I16)


def join_table(device, me, key_slot, perm):
    first = device * 4
    owner = (key_slot[pl.ds(first, 4), :] >> 11).astype(F32)
    across = jnp.concatenate([owner[j : j + 1] for j in range(4)], axis=1)
    down = jnp.concatenate([owner, owner], axis=0).T
    index = iota((LANES, KEY_DEV), 1)
    for j in range(4):
        column = down[:, j : j + 1]
        earlier = index < iota((LANES, KEY_DEV), 0) + j * LANES
        same = jnp.where((column == across) & earlier, 1.0, 0.0)
        rank = jnp.sum(same, axis=1, keepdims=True).astype(I32)
        step = (me - column.astype(I32)) & (MEMBERS - 1)
        perm[j * LANES : (j + 1) * LANES, :] = onehot(step * KPP + rank == index)


def fused(
    heavy, keys, heavy_row, key_slot, measures_hbm, orders_hbm,
    result, report, slot_rows,
    measures, pairs, orders, slots, heavy_spot, seg, ranks_hist, heavy_hist, meta,
    send, got, side, got_side, acc, sp, spread, local, rank, perm,
    out2, in2, out3, in3, totals, hist,
    hv_sums, hv_in, hm_out, hm_in, slot_out, slot_in,
    local_sem, s_main, r_main, s_side, r_side, s_two, r_two, s_three, r_three,
    s_hv, r_hv, s_hm, r_hm, s_slot, r_slot,
):
    me_x, me_y = lax.axis_index("gx"), lax.axis_index("gy")
    device = me_x * GY + me_y
    me, group = member_of(device)
    barrier = pltpu.get_barrier_semaphore()
    fetch = pltpu.make_async_copy(measures_hbm, measures, local_sem.at[0])
    fetch.start()
    fetch_orders = pltpu.make_async_copy(orders_hbm, orders, local_sem.at[1])
    fetch_orders.start()

    def place(member, its_group):
        x, y = member >> 4, (member >> 2) & 3
        return (x * 8 + its_group * 2 + ((member >> 1) & 1)) * 2 + (member & 1), y

    def along(s):
        return lax.rem(me + s, MEMBERS)

    def in_group(s):
        return place(along(s), group)

    def across(s):
        return place(me, lax.rem(group + s, GROUPS))

    opposite = (me, group)
    alone = group == me_y

    def copy(src, dst, send_sem, recv_sem, s, target):
        return pltpu.make_async_remote_copy(
            src_ref=src, dst_ref=dst, send_sem=send_sem.at[s], recv_sem=recv_sem.at[s],
            device_id=target, device_id_type=MESH,
        )

    def main_copy(s):
        return copy(send.at[s], got.at[s], s_main, r_main, s, in_group(s))

    def side_copy(s):
        return copy(side.at[s], got_side.at[s], s_side, r_side, s, in_group(s))

    def heavy_copy(s):
        return copy(hv_sums.at[lax.rem(group + s, GROUPS)], hv_in.at[s], s_hv, r_hv, s, across(s))

    def member_copy(s):
        return copy(hm_out.at[along(s)], hm_in.at[s], s_hm, r_hm, s, in_group(s))

    def two_copy(s):
        return copy(out2.at[s], in2.at[s], s_two, r_two, s, across(s))

    def three_copy(s):
        return copy(out3.at[along(s)], in3.at[s], s_three, r_three, s, in_group(s))

    def slot_copy():
        return copy(slot_out, slot_in, s_slot, r_slot, 0, opposite)

    @pl.loop(1, MEMBERS)
    def _(s):
        pl.semaphore_signal(barrier, inc=1, device_id=in_group(s), device_id_type=MESH)

    for s in range(1, GROUPS):
        pl.semaphore_signal(barrier, inc=1, device_id=across(s), device_id_type=MESH)

    @pl.when(jnp.logical_not(alone))
    def _():
        pl.semaphore_signal(barrier, inc=1, device_id=opposite, device_id_type=MESH)

    def pair_sums(spots):
        total = jnp.zeros((CHUNK, 2 * LANES), F32)
        for b in range(ROWS // BLOCK):
            span = slice(b * BLOCK, (b + 1) * BLOCK)
            total = total + dot(hot16(CHUNK, spread16(spots(span))), pairs[span, :])
        return total

    find_slots(keys, heavy_row, key_slot, slots, heavy_spot, ranks_hist, heavy_hist)
    fetch.wait()
    find_ranks(me, slots, heavy_spot, seg, ranks_hist, meta, side, measures, pairs)

    @pl.when(alone)
    def _():
        pl.semaphore_wait(barrier, MEMBERS - 1 + GROUPS - 1)

    @pl.when(jnp.logical_not(alone))
    def _():
        pl.semaphore_wait(barrier, MEMBERS + GROUPS - 1)

    left = iota((1, LANES), 1) < CAPK
    lane = iota((HALF, LANES), 1) & (CAPK - 1)
    lower_lane = lane == iota((HALF, LANES), 0)
    upper_lane = lane == iota((HALF, LANES), 0) + HALF

    def start_chunk(c):
        @pl.loop(jnp.maximum(c * STEPS, 1), (c + 1) * STEPS)
        def _(s):
            main_copy(s).start()
            side_copy(s).start()

    @pl.loop(0, CHUNKS)
    def _(c):
        total = pair_sums(lambda span: seg[:, span] - c * CHUNK)
        lower, lower_power = power_of(total[:, :LANES])
        upper, upper_power = power_of(total[:, LANES:])
        for i in range(STEPS):
            s = c * STEPS + i
            at = slice(i * HALF, (i + 1) * HALF)
            powers = jnp.where(lower_lane, lower_power[at], 0.0)
            powers = powers + jnp.where(upper_lane, upper_power[at], 0.0)
            send[s, 0:HALF] = lower[at].astype(I16)
            send[s, HALF:CAPK] = upper[at].astype(I16)
            side[s, 2:3] = jnp.exp2(jnp.sum(powers, axis=0, keepdims=True))

        @pl.when(c == 0)
        def _():
            got[0] = send[0]
            got_side[0] = side[0]
            for h in range(HPG * GROUPS // HPD // CHUNK):
                both = pair_sums(
                    lambda span: jnp.where(heavy_spot[:, span] < 0, -1, heavy_spot[:, span] >> 1)
                    - h * CHUNK
                )
                for k in range(CHUNK // MEMBERS):
                    at = slice(k * MEMBERS, (k + 1) * MEMBERS)
                    n = h * (CHUNK // MEMBERS) + k
                    hv_sums[n, 0:MEMBERS] = both[at, :LANES]
                    hv_sums[n, MEMBERS:HPG] = both[at, LANES:]
                    hv_sums[n, HPG : HPG + 8] = jnp.broadcast_to(
                        heavy_hist[n : n + 1, :], (8, LANES)
                    )

        @pl.when(c > 0)
        def _():
            start_chunk(c - 1)

        @pl.when(c == 1)
        def _():
            for s in range(1, GROUPS):
                heavy_copy(s).start()

        @pl.when(c == CHUNKS // 2)
        def _():
            total = hv_sums[group]
            for s in range(1, GROUPS):
                heavy_copy(s).wait_recv()
                total = total + hv_in[s]
            for m in range(MEMBERS):
                rows = [total[h * MEMBERS + m : h * MEMBERS + m + 1] for h in range(HPD)]
                rows.append(total[HPG : HPG + 2])
                hm_out[m] = jnp.concatenate(rows, axis=0)

    owner_table(me, key_slot, local, rank, spread, sp)
    start_chunk(CHUNKS - 1)

    @pl.loop(1, MEMBERS)
    def _(s):
        member_copy(s).start()

    join_table(device, me, key_slot, perm)
    acc[...] = jnp.zeros(acc.shape, F32)
    hist[...] = jnp.zeros(hist.shape, F32)

    @pl.loop(0, CHUNKS)
    def _(g):
        @pl.loop(jnp.maximum(g * STEPS, 1), (g + 1) * STEPS)
        def _(s):
            main_copy(s).wait_recv()
            side_copy(s).wait_recv()

        hots, wanted, counts = [], [], []
        for j in range(STEPS // 2):
            s = g * STEPS + 2 * j
            rows = jnp.where(left, got_side[s], got_side[s + 1])
            slot = rows[1:2].astype(I32)
            wanted.append(slot)
            counts.append(rows[0:1])
            target = jnp.broadcast_to(slot, (16, LANES)).astype(I16)
            one = value16(rows[2:3])
            zero = jnp.zeros((16, LANES), BF16)
            hots.append(
                jnp.concatenate(
                    [
                        jnp.where(sp[16 * t : 16 * t + 16, :] == target, one, zero)
                        for t in range(OWN // 16)
                    ],
                    axis=0,
                )
            )
        rows = got[pl.ds(g * STEPS, STEPS)].reshape(STEPS * CAPK, LANES).astype(I32)
        pieces = [(rows >> 8).astype(F32).astype(BF16), (rows & 255).astype(F32).astype(BF16)]
        found = dot(jnp.concatenate(hots, axis=1), jnp.concatenate(pieces, axis=1))
        acc[...] += found[:, :LANES] * (256.0 / FULL) + found[:, LANES:] * (1.0 / FULL)
        slot = jnp.concatenate(wanted, axis=1)
        count = value16(jnp.concatenate(counts, axis=1))
        hist[...] += dot(
            hot16(OWN_ROWS, spread16(slot >> 7)), hot16(LANES, spread16(slot & 127), count), NT
        )

    def part_of(q):
        return pl.ds(pl.multiple_of(q * KEY_DEV, KEY_DEV), KEY_DEV)

    slot_total = hist[...]
    for s in range(1, GROUPS):
        fixed, exponents = encode(acc[part_of(lax.rem(group + s, GROUPS)), :])
        extra = jnp.concatenate(
            [slot_total, *exponents, jnp.zeros((EXTRA - OWN_ROWS - 4, LANES), F32)], axis=0
        )
        out2[s, KEY_DEV : KEY_DEV + EXTRA] = extra.astype(I32).astype(I16)
        out2[s, 0:KEY_DEV] = fixed.astype(I16)
        if s > 1:
            two_copy(s - 1).start()
    slot = sp[part_of(group), :].astype(I32)
    totals[...] = acc[part_of(group), :]
    two_copy(GROUPS - 1).start()
    hm_in[0] = hm_out[me]

    @pl.loop(1, MEMBERS)
    def _(s):
        main_copy(s).wait_send()
        side_copy(s).wait_send()
        member_copy(s).wait_send()
        member_copy(s).wait_recv()

    heavy_total = jnp.sum(hm_in[...], axis=0)
    for s in range(1, GROUPS):
        two_copy(s).wait_recv()
        part = in2[s, KEY_DEV : KEY_DEV + EXTRA].astype(I32).astype(F32)
        slot_total = slot_total + part[0:OWN_ROWS]
        for j in range(4):
            at = slice(j * LANES, (j + 1) * LANES)
            scale = scales_down(part[OWN_ROWS + j : OWN_ROWS + 1 + j], LANES, 0)
            totals[at, :] += in2[s, at].astype(I32).astype(F32) * scale
    hist[...] = slot_total
    slot_out[...] = hist[pl.ds(group * 4, 4), :]
    wide = jnp.zeros((KEY_DEV, LANES), F32)
    for r in range(OWN_ROWS):
        wide = wide + jnp.where(slot >> 7 == r, slot_total[r : r + 1], 0.0)
    wide = jnp.where((slot & 127) == iota((KEY_DEV, LANES), 1), wide, 0.0)
    count = jnp.sum(wide, axis=1, keepdims=True)
    totals[...] = totals[...] * lax.rsqrt(1.0 + count)
    for m in range(MEMBERS):
        out3[m] = totals[m * KPP : (m + 1) * KPP, :]
    in3[0] = totals[pl.ds(pl.multiple_of(me * KPP, KPP), KPP), :]
    lane = iota((1, LANES), 1)
    sized = []
    for h in range(HPD):
        number = jnp.sum(
            jnp.where(lane == me * HPD + h, heavy_total[HPD : HPD + 1], 0.0),
            axis=1, keepdims=True,
        )
        sized.append(heavy_total[h : h + 1] * lax.rsqrt(1.0 + number))

    @pl.loop(1, MEMBERS)
    def _(s):
        three_copy(s).start()

    @pl.when(alone)
    def _():
        slot_rows[...] = slot_out[...]

    @pl.when(jnp.logical_not(alone))
    def _():
        slot_copy().start()

    line = iota((KEY_DEV, LANES), 0)
    fetch_orders.wait()
    attributes = orders[...].astype(F32)
    heavy_part = jnp.zeros((KEY_DEV, LANES), F32)
    lines = []
    for h in range(HPD):
        spot = heavy[device * HPD + h] - device * KEY_DEV
        here = line == spot
        heavy_part = heavy_part + jnp.where(here, sized[h], 0.0)
        lines.append(jnp.sum(jnp.where(here, attributes, 0.0), axis=0, keepdims=True) * sized[h])
    report[...] = jnp.concatenate(lines, axis=0).astype(BF16)
    totals[...] = heavy_part
    for s in range(1, GROUPS):
        two_copy(s).wait_send()
        heavy_copy(s).wait_send()

    @pl.when(jnp.logical_not(alone))
    def _():
        slot_copy().wait_send()
        slot_copy().wait_recv()
        slot_rows[...] = slot_in[...]

    @pl.loop(1, MEMBERS)
    def _(s):
        three_copy(s).wait_recv()

    rows = in3[...].reshape(KEY_DEV, LANES)
    high = rows.astype(BF16)
    low = (rows - high.astype(F32)).astype(BF16)
    both = dot(perm[...], jnp.concatenate([high, low], axis=1))
    found = both[:, :LANES] + both[:, LANES:] + totals[...]
    result[...] = (orders[...].astype(F32) * found).astype(BF16)

    @pl.loop(1, MEMBERS)
    def _(s):
        three_copy(s).wait_send()


def hand_on(*refs):
    half = len(refs) // 2
    for source, target in zip(refs[:half], refs[half:]):
        target[...] = source[...]


def shaped(*dims, dtype=F32):
    return jax.ShapeDtypeStruct(dims, dtype)


def body(measures, row_keys, orders, heavy_keys, key_slot):
    table = key_slot.reshape(key_slot.shape[0] // LANES, LANES)
    dma = pltpu.SemaphoreType.DMA
    outs = (
        shaped(KEY_DEV, LANES, dtype=BF16),
        shaped(HPD, LANES, dtype=BF16),
        shaped(KEY_DEV // LANES, LANES),
    )
    found = pl.pallas_call(
        fused,
        out_shape=outs,
        in_specs=[SMEM] + [VMEM] * 3 + [ANY] * 2,
        out_specs=(VMEM,) * 3,
        scratch_shapes=[
            pltpu.VMEM((ROWS, LANES), BF16),
            pltpu.VMEM((ROWS, 2 * LANES), BF16),
            pltpu.VMEM((KEY_DEV, LANES), BF16),
            pltpu.VMEM((1, ROWS), I32),
            pltpu.VMEM((1, ROWS), I32),
            pltpu.VMEM((1, ROWS), I32),
            pltpu.VMEM((512, 256), F32),
            pltpu.VMEM((16, LANES), F32),
            pltpu.VMEM((256, LANES), F32),
            pltpu.VMEM((MEMBERS, CAPK, LANES), I16),
            pltpu.VMEM((MEMBERS, CAPK, LANES), I16),
            pltpu.VMEM((MEMBERS, 4, LANES), F32),
            pltpu.VMEM((MEMBERS, 4, LANES), F32),
            pltpu.VMEM((OWN, LANES), F32),
            pltpu.VMEM((OWN, LANES), I16),
            pltpu.VMEM((OWN, LANES), F32),
            pltpu.VMEM((1024, LANES), F32),
            pltpu.VMEM((1024, LANES), F32),
            pltpu.VMEM((KEY_DEV, KEY_DEV), BF16),
            pltpu.VMEM((GROUPS, KEY_DEV + EXTRA, LANES), I16),
            pltpu.VMEM((GROUPS, KEY_DEV + EXTRA, LANES), I16),
            pltpu.VMEM((MEMBERS, KPP, LANES), F32),
            pltpu.VMEM((MEMBERS, KPP, LANES), F32),
            pltpu.VMEM((KEY_DEV, LANES), F32),
            pltpu.VMEM((OWN_ROWS, LANES), F32),
            pltpu.VMEM((GROUPS, HPG + 8, LANES), F32),
            pltpu.VMEM((GROUPS, HPG + 8, LANES), F32),
            pltpu.VMEM((MEMBERS, 4, LANES), F32),
            pltpu.VMEM((MEMBERS, 4, LANES), F32),
            pltpu.VMEM((4, LANES), F32),
            pltpu.VMEM((4, LANES), F32),
            dma((2,)),
        ]
        + [dma((MEMBERS,))] * 4
        + [dma((GROUPS,))] * 2
        + [dma((MEMBERS,))] * 2
        + [dma((GROUPS,))] * 2
        + [dma((MEMBERS,))] * 2
        + [dma((1,))] * 2,
        compiler_params=pltpu.CompilerParams(
            collective_id=0, has_side_effects=True, vmem_limit_bytes=LIMIT
        ),
    )(heavy_keys, row_keys.reshape(1, ROWS), heavy_keys.reshape(1, -1), table, measures, orders)
    result, report, slot_rows = pl.pallas_call(
        hand_on,
        out_shape=outs,
        in_specs=[VMEM] * 3,
        out_specs=(VMEM,) * 3,
    )(*found)
    return (result, report, slot_rows.reshape(KEY_DEV))


def solution(mesh):
    return jax.shard_map(
        body,
        mesh=mesh,
        in_specs=(P(("gx", "gy"), None), P(("gx", "gy")), P(("gx", "gy"), None), P(), P()),
        out_specs=(P(("gx", "gy"), None), P(("gx", "gy"), None), P(("gx", "gy"))),
        check_vma=False,
    )
```

time: 94.6 us -> 85.2 us (0.901)
  Pallas kernels: 89.7 us -> 84.4 us
  local copies, waits for them, and re-layouts: 4.01 us -> 0 us
    pallas_call x2, Pallas kernels: 89.7 us -> 84.4 us  [the longest x1 82.8 us: body(): pl.pallas_call(fused, out_shape=outs, in_specs=[SMEM] + [VMEM] * 3 + [ANY...]
    unnamed x3 -> x0, local copies, waits for them, and re-layouts: 4.01 us -> none
where the time goes in v1:
time: 85.2 us; the launch traced here: 85 us
  Pallas kernels  84.4 us (99%)
    pallas_call x1, Pallas kernels, body(): pl.pallas_call(fused, out_shape=outs, in_specs=[SMEM] + [VMEM] * 3 + [ANY...  82.8 us

profile of v1, /device:TPU:1, one launch (start us, length us, event | category | flops | bytes accessed | tf_op | source)
XLA Modules:
  0.0 85.0 jit_solution(5988682356332803397)
XLA Ops:
  0.6 82.8 %shard_map.76 = (bf16[512,128]{1,0:T(8,128)(2,1)}, bf16[2,128]{1,0:T(2,128)(2,1)}, f32[4,128]{1,0:T(4,128)}) custom-call(s32[512]{0:T(512)} %heavy.1, s32[1,8192]{1,0:T(1,128)} %bitcast.5, s32[1,512]{1,0:T(1,128)} %bitcast.6, s32[1024,128]{1,0:T(8,128)} %bitcast.4, bf16[8192,128]{1,0:T(8,128)(2,1)} %measures_hbm.1, bf16[512,128]{1,0:T(8,128)(2,1)} %orders_hbm.1), custom_call_target="tpu_custom_call" | custom-call | tf_op jit(solution)/shard_map/pallas_call | solution.py:568
  83.5 1.6 %shard_map.77 = (bf16[512,128]{1,0:T(8,128)(2,1)}, bf16[2,128]{1,0:T(2,128)(2,1)}, f32[4,128]{1,0:T(4,128)}) custom-call(bf16[512,128]{1,0:T(8,128)(2,1)} %get-tuple-element.9.refs_0_, bf16[2,128]{1,0:T(2,128)(2,1)} %get-tuple-element.10.refs_1_, f32[4,128]{1,0:T(4,128)} %get-tuple-element.11.refs_2_), custom_call_target="tpu_custom_call" | custom-call | tf_op jit(solution)/shard_map/pallas_call | solution.py:617

commit v2 on v1

--- a/solution.py
+++ b/solution.py
@@ -32,9 +32,11 @@
 HPD = 2
 HPG = HPD * MEMBERS
 STEPS = 8
+TAKEN = 8
 HALF = CAPK // 2
 CHUNK = STEPS * HALF
 CHUNKS = MEMBERS // STEPS
+DESCRIBED = 1 if STEPS == 8 else 0
 EXTRA = 32
 FULL = 32000.0
 
@@ -137,7 +139,7 @@
         )
 
 
-def find_ranks(me, slots, heavy_spot, seg_out, hist, meta, side, measures, pairs):
+def find_ranks(me, slots, heavy_spot, seg_out, places, hist, measures, pairs):
     present = hist[...] > 0.0
     flag = onehot(present)
     inside = dot(flag, onehot(iota((256, 256), 0) < iota((256, 256), 1)))
@@ -146,7 +148,6 @@
     before = dot(onehot((col < row) & (col >> 3 == row >> 3)), whole.astype(BF16))
     rank = inside + jnp.concatenate([before, before], axis=1)
     ranks = jnp.where(present, rank, 0.0).T.astype(BF16)
-    meta[...] = jnp.zeros(meta.shape, F32)
     low_index = iota((256, BLOCK), 0)
 
     @pl.loop(0, ROWS // BLOCK)
@@ -156,6 +157,7 @@
         light = slot >= 0
         wide = dot(ranks, hot16(512, spread16(slot >> 8)))
         place = pick(wide, low_index == (slot & 255)).astype(I32)
+        places[:, span] = jnp.where(light, place, -1)
         step = ((slot >> 11) - me) & (MEMBERS - 1)
         seg_out[:, span] = jnp.where(light, step * HALF + (place & (HALF - 1)), -1)
         bit = jnp.where(light, place >> 5, heavy_spot[:, span] & 1).astype(F32)
@@ -167,7 +169,16 @@
             upper = rows * jnp.broadcast_to(down[:, i : i + 1], (LANES, LANES)).astype(BF16)
             pairs[at, LANES:] = upper
             pairs[at, :LANES] = rows - upper
-        base = spread16(jnp.where(light, place, -1))
+
+
+def describe(me, slots, places, meta, packed):
+    meta[...] = jnp.zeros(meta.shape, F32)
+
+    @pl.loop(0, ROWS // BLOCK)
+    def _(b):
+        span = pl.ds(pl.multiple_of(b * BLOCK, BLOCK), BLOCK)
+        slot = slots[:, span]
+        base = spread16(places[:, span])
         kinds = jnp.concatenate(
             [
                 hot16(64, base),
@@ -176,24 +187,16 @@
             ],
             axis=0,
         )
-        meta[0:192, :] += dot(kinds, hot16(LANES, spread16(jnp.where(light, step, -1))), NT)
+        step = jnp.where(slot >= 0, ((slot >> 11) - me) & (MEMBERS - 1), -1)
+        meta[0:192, :] += dot(kinds, hot16(LANES, spread16(step)), NT)
 
     turn = meta[...].T
-    left = iota((MEMBERS, LANES), 1) < CAPK
-
-    def doubled(pair):
-        swapped = pltpu.roll(pair, CAPK, 1)
-        return jnp.where(left, pair, swapped), jnp.where(left, swapped, pair)
-
-    count, low_sum = doubled(turn[:MEMBERS, :LANES])
-    high_sum, unused = doubled(turn[:MEMBERS, LANES:])
+    count, high_sum = turn[:MEMBERS, :LANES], turn[:MEMBERS, LANES:]
+    low_sum = pltpu.roll(count, CAPK, 1)
     share = 1.0 / jnp.maximum(count, 1.0)
     low_slot = jnp.floor(low_sum * share + 0.5)
     high_slot = jnp.floor(high_sum * share + 0.5)
-    slot = jnp.where(count > 0.0, high_slot * 256.0 + low_slot, -1.0)
-    side[:, 0, :] = count
-    side[:, 1, :] = slot
-    side[:, 3, :] = jnp.zeros((MEMBERS, LANES), F32)
+    packed[...] = count * OWN + high_slot * 256.0 + low_slot
 
 
 def owner_table(me, key_slot, local, rank, spread, sp):
@@ -242,9 +245,9 @@
 
 
 def fused(
-    heavy, keys, heavy_row, key_slot, measures_hbm, orders_hbm,
+    heavy, keys, heavy_row, key_slot_hbm, measures_hbm, orders_hbm,
     result, report, slot_rows,
-    measures, pairs, orders, slots, heavy_spot, seg, ranks_hist, heavy_hist, meta,
+    key_slot, measures, pairs, orders, slots, heavy_spot, seg, places, packed, scales, ranks_hist, heavy_hist, meta,
     send, got, side, got_side, acc, sp, spread, local, rank, perm,
     out2, in2, out3, in3, totals, hist,
     hv_sums, hv_in, hm_out, hm_in, slot_out, slot_in,
@@ -255,6 +258,8 @@
     device = me_x * GY + me_y
     me, group = member_of(device)
     barrier = pltpu.get_barrier_semaphore()
+    fetch_slots = pltpu.make_async_copy(key_slot_hbm, key_slot, local_sem.at[2])
+    fetch_slots.start()
     fetch = pltpu.make_async_copy(measures_hbm, measures, local_sem.at[0])
     fetch.start()
     fetch_orders = pltpu.make_async_copy(orders_hbm, orders, local_sem.at[1])
@@ -303,8 +308,7 @@
     def slot_copy():
         return copy(slot_out, slot_in, s_slot, r_slot, 0, opposite)
 
-    @pl.loop(1, MEMBERS)
-    def _(s):
+    for s in range(1, MEMBERS):
         pl.semaphore_signal(barrier, inc=1, device_id=in_group(s), device_id_type=MESH)
 
     for s in range(1, GROUPS):
@@ -314,16 +318,17 @@
     def _():
         pl.semaphore_signal(barrier, inc=1, device_id=opposite, device_id_type=MESH)
 
-    def pair_sums(spots):
-        total = jnp.zeros((CHUNK, 2 * LANES), F32)
+    def pair_sums(count, spots):
+        total = jnp.zeros((count, 2 * LANES), F32)
         for b in range(ROWS // BLOCK):
             span = slice(b * BLOCK, (b + 1) * BLOCK)
-            total = total + dot(hot16(CHUNK, spread16(spots(span))), pairs[span, :])
+            total = total + dot(hot16(count, spread16(spots(span))), pairs[span, :])
         return total
 
+    fetch_slots.wait()
     find_slots(keys, heavy_row, key_slot, slots, heavy_spot, ranks_hist, heavy_hist)
     fetch.wait()
-    find_ranks(me, slots, heavy_spot, seg, ranks_hist, meta, side, measures, pairs)
+    find_ranks(me, slots, heavy_spot, seg, places, ranks_hist, measures, pairs)
 
     @pl.when(alone)
     def _():
@@ -338,15 +343,18 @@
     lower_lane = lane == iota((HALF, LANES), 0)
     upper_lane = lane == iota((HALF, LANES), 0) + HALF
 
-    def start_chunk(c):
+    def start_sides(c):
+        for i in range(STEPS):
+            s = c * STEPS + i
+            side[s] = jnp.where(left, packed[pl.ds(s, 1), :], scales[s])
+
         @pl.loop(jnp.maximum(c * STEPS, 1), (c + 1) * STEPS)
         def _(s):
-            main_copy(s).start()
             side_copy(s).start()
 
     @pl.loop(0, CHUNKS)
     def _(c):
-        total = pair_sums(lambda span: seg[:, span] - c * CHUNK)
+        total = pair_sums(CHUNK, lambda span: seg[:, span] - c * CHUNK)
         lower, lower_power = power_of(total[:, :LANES])
         upper, upper_power = power_of(total[:, LANES:])
         for i in range(STEPS):
@@ -356,73 +364,77 @@
             powers = powers + jnp.where(upper_lane, upper_power[at], 0.0)
             send[s, 0:HALF] = lower[at].astype(I16)
             send[s, HALF:CAPK] = upper[at].astype(I16)
-            side[s, 2:3] = jnp.exp2(jnp.sum(powers, axis=0, keepdims=True))
-
-        @pl.when(c == 0)
+            scales[s] = jnp.exp2(jnp.sum(powers, axis=0, keepdims=True))
+
+        @pl.loop(jnp.maximum(c * STEPS, 1), (c + 1) * STEPS)
+        def _(s):
+            main_copy(s).start()
+
+        @pl.when(c == DESCRIBED)
         def _():
+            describe(me, slots, places, meta, packed)
+            for n in range(DESCRIBED):
+                start_sides(n)
             got[0] = send[0]
-            got_side[0] = side[0]
-            for h in range(HPG * GROUPS // HPD // CHUNK):
-                both = pair_sums(
-                    lambda span: jnp.where(heavy_spot[:, span] < 0, -1, heavy_spot[:, span] >> 1)
-                    - h * CHUNK
-                )
-                for k in range(CHUNK // MEMBERS):
-                    at = slice(k * MEMBERS, (k + 1) * MEMBERS)
-                    n = h * (CHUNK // MEMBERS) + k
-                    hv_sums[n, 0:MEMBERS] = both[at, :LANES]
-                    hv_sums[n, MEMBERS:HPG] = both[at, LANES:]
-                    hv_sums[n, HPG : HPG + 8] = jnp.broadcast_to(
-                        heavy_hist[n : n + 1, :], (8, LANES)
-                    )
-
-        @pl.when(c > 0)
+
+        @pl.when(c >= DESCRIBED)
         def _():
-            start_chunk(c - 1)
-
-        @pl.when(c == 1)
+            start_sides(c)
+
+        @pl.when(c == DESCRIBED + 1)
+        def _():
+            both = pair_sums(
+                MEMBERS * GROUPS,
+                lambda span: jnp.where(heavy_spot[:, span] < 0, -1, heavy_spot[:, span] >> 1),
+            )
+            for n in range(GROUPS):
+                at = slice(n * MEMBERS, (n + 1) * MEMBERS)
+                hv_sums[n, 0:MEMBERS] = both[at, :LANES]
+                hv_sums[n, MEMBERS:HPG] = both[at, LANES:]
+                hv_sums[n, HPG : HPG + 8] = jnp.broadcast_to(heavy_hist[n : n + 1, :], (8, LANES))
+
+        @pl.when(c == DESCRIBED + 2)
         def _():
             for s in range(1, GROUPS):
                 heavy_copy(s).start()
 
-        @pl.when(c == CHUNKS // 2)
-        def _():
-            total = hv_sums[group]
-            for s in range(1, GROUPS):
-                heavy_copy(s).wait_recv()
-                total = total + hv_in[s]
-            for m in range(MEMBERS):
-                rows = [total[h * MEMBERS + m : h * MEMBERS + m + 1] for h in range(HPD)]
-                rows.append(total[HPG : HPG + 2])
-                hm_out[m] = jnp.concatenate(rows, axis=0)
-
+    got_side[0] = side[0]
     owner_table(me, key_slot, local, rank, spread, sp)
-    start_chunk(CHUNKS - 1)
+
+    total = hv_sums[group]
+    for s in range(1, GROUPS):
+        heavy_copy(s).wait_recv()
+        total = total + hv_in[s]
+    for m in range(MEMBERS):
+        rows = [total[h * MEMBERS + m : h * MEMBERS + m + 1] for h in range(HPD)]
+        rows.append(total[HPG : HPG + 2])
+        hm_out[m] = jnp.concatenate(rows, axis=0)
+    join_table(device, me, key_slot, perm)
 
     @pl.loop(1, MEMBERS)
     def _(s):
         member_copy(s).start()
 
-    join_table(device, me, key_slot, perm)
     acc[...] = jnp.zeros(acc.shape, F32)
     hist[...] = jnp.zeros(hist.shape, F32)
 
-    @pl.loop(0, CHUNKS)
+    @pl.loop(0, MEMBERS // TAKEN)
     def _(g):
-        @pl.loop(jnp.maximum(g * STEPS, 1), (g + 1) * STEPS)
+        @pl.loop(jnp.maximum(g * TAKEN, 1), (g + 1) * TAKEN)
         def _(s):
             main_copy(s).wait_recv()
             side_copy(s).wait_recv()
 
         hots, wanted, counts = [], [], []
-        for j in range(STEPS // 2):
-            s = g * STEPS + 2 * j
-            rows = jnp.where(left, got_side[s], got_side[s + 1])
-            slot = rows[1:2].astype(I32)
+        for j in range(TAKEN // 2):
+            s = g * TAKEN + 2 * j
+            a, b = got_side[s], got_side[s + 1]
+            entry = jnp.where(left, a, pltpu.roll(b, CAPK, 1)).astype(I32)
+            slot = jnp.where(entry >= OWN, entry & (OWN - 1), -1)
             wanted.append(slot)
-            counts.append(rows[0:1])
+            counts.append((entry >> 11).astype(F32))
             target = jnp.broadcast_to(slot, (16, LANES)).astype(I16)
-            one = value16(rows[2:3])
+            one = value16(jnp.where(left, pltpu.roll(a, CAPK, 1), b))
             zero = jnp.zeros((16, LANES), BF16)
             hots.append(
                 jnp.concatenate(
@@ -433,10 +445,11 @@
                     axis=0,
                 )
             )
-        rows = got[pl.ds(g * STEPS, STEPS)].reshape(STEPS * CAPK, LANES).astype(I32)
-        pieces = [(rows >> 8).astype(F32).astype(BF16), (rows & 255).astype(F32).astype(BF16)]
+        rows = got[pl.ds(g * TAKEN, TAKEN)].reshape(TAKEN * CAPK, LANES).astype(I32)
+        low = rows & 255
+        pieces = [(rows - low).astype(F32).astype(BF16), low.astype(F32).astype(BF16)]
         found = dot(jnp.concatenate(hots, axis=1), jnp.concatenate(pieces, axis=1))
-        acc[...] += found[:, :LANES] * (256.0 / FULL) + found[:, LANES:] * (1.0 / FULL)
+        acc[...] += found[:, :LANES] + found[:, LANES:]
         slot = jnp.concatenate(wanted, axis=1)
         count = value16(jnp.concatenate(counts, axis=1))
         hist[...] += dot(
@@ -484,7 +497,7 @@
         wide = wide + jnp.where(slot >> 7 == r, slot_total[r : r + 1], 0.0)
     wide = jnp.where((slot & 127) == iota((KEY_DEV, LANES), 1), wide, 0.0)
     count = jnp.sum(wide, axis=1, keepdims=True)
-    totals[...] = totals[...] * lax.rsqrt(1.0 + count)
+    totals[...] = totals[...] * (lax.rsqrt(1.0 + count) * (1.0 / FULL))
     for m in range(MEMBERS):
         out3[m] = totals[m * KPP : (m + 1) * KPP, :]
     in3[0] = totals[pl.ds(pl.multiple_of(me * KPP, KPP), KPP), :]
@@ -497,8 +510,7 @@
         )
         sized.append(heavy_total[h : h + 1] * lax.rsqrt(1.0 + number))
 
-    @pl.loop(1, MEMBERS)
-    def _(s):
+    for s in range(1, MEMBERS):
         three_copy(s).start()
 
     @pl.when(alone)
@@ -568,22 +580,26 @@
     found = pl.pallas_call(
         fused,
         out_shape=outs,
-        in_specs=[SMEM] + [VMEM] * 3 + [ANY] * 2,
+        in_specs=[SMEM] + [VMEM] * 2 + [ANY] * 3,
         out_specs=(VMEM,) * 3,
         scratch_shapes=[
+            pltpu.VMEM((KEY_DEV * MEMBERS * GROUPS // LANES, LANES), I32),
             pltpu.VMEM((ROWS, LANES), BF16),
             pltpu.VMEM((ROWS, 2 * LANES), BF16),
             pltpu.VMEM((KEY_DEV, LANES), BF16),
             pltpu.VMEM((1, ROWS), I32),
             pltpu.VMEM((1, ROWS), I32),
             pltpu.VMEM((1, ROWS), I32),
+            pltpu.VMEM((1, ROWS), I32),
+            pltpu.VMEM((MEMBERS, LANES), F32),
+            pltpu.VMEM((MEMBERS, 1, LANES), F32),
             pltpu.VMEM((512, 256), F32),
             pltpu.VMEM((16, LANES), F32),
             pltpu.VMEM((256, LANES), F32),
             pltpu.VMEM((MEMBERS, CAPK, LANES), I16),
             pltpu.VMEM((MEMBERS, CAPK, LANES), I16),
-            pltpu.VMEM((MEMBERS, 4, LANES), F32),
-            pltpu.VMEM((MEMBERS, 4, LANES), F32),
+            pltpu.VMEM((MEMBERS, 1, LANES), F32),
+            pltpu.VMEM((MEMBERS, 1, LANES), F32),
             pltpu.VMEM((OWN, LANES), F32),
             pltpu.VMEM((OWN, LANES), I16),
             pltpu.VMEM((OWN, LANES), F32),
@@ -602,7 +618,7 @@
             pltpu.VMEM((MEMBERS, 4, LANES), F32),
             pltpu.VMEM((4, LANES), F32),
             pltpu.VMEM((4, LANES), F32),
-            dma((2,)),
+            dma((3,)),
         ]
         + [dma((MEMBERS,))] * 4
         + [dma((GROUPS,))] * 2

time: 85.2 us -> 82.2 us (0.965)
  Pallas kernels: 84.4 us -> 81.3 us
    pallas_call x1, Pallas kernels: 82.8 us -> 79.8 us  [body(): pl.pallas_call(fused, out_shape=outs, in_specs=[SMEM] + [VMEM] * 2 + [ANY...]
where the time goes in v2:
time: 82.2 us; the launch traced here: 82 us
  Pallas kernels  81.3 us (99%)
    pallas_call x1, Pallas kernels, body(): pl.pallas_call(fused, out_shape=outs, in_specs=[SMEM] + [VMEM] * 2 + [ANY...  79.8 us

profile of v2, /device:TPU:1, one launch (start us, length us, event | category | flops | bytes accessed | tf_op | source)
XLA Modules:
  0.0 82.0 jit_solution(9708831675253222643)
XLA Ops:
  0.6 79.8 %shard_map.76 = (bf16[512,128]{1,0:T(8,128)(2,1)}, bf16[2,128]{1,0:T(2,128)(2,1)}, f32[4,128]{1,0:T(4,128)}) custom-call(s32[512]{0:T(512)} %heavy.1, s32[1,8192]{1,0:T(1,128)} %bitcast.5, s32[1,512]{1,0:T(1,128)} %bitcast.6, s32[1024,128]{1,0:T(8,128)} %bitcast.4, bf16[8192,128]{1,0:T(8,128)(2,1)} %measures_hbm.1, bf16[512,128]{1,0:T(8,128)(2,1)} %orders_hbm.1), custom_call_target="tpu_custom_call" | custom-call | tf_op jit(solution)/shard_map/pallas_call | solution.py:580
  80.4 1.6 %shard_map.77 = (bf16[512,128]{1,0:T(8,128)(2,1)}, bf16[2,128]{1,0:T(2,128)(2,1)}, f32[4,128]{1,0:T(4,128)}) custom-call(bf16[512,128]{1,0:T(8,128)(2,1)} %get-tuple-element.9.refs_0_, bf16[2,128]{1,0:T(2,128)(2,1)} %get-tuple-element.10.refs_1_, f32[4,128]{1,0:T(4,128)} %get-tuple-element.11.refs_2_), custom_call_target="tpu_custom_call" | custom-call | tf_op jit(solution)/shard_map/pallas_call | solution.py:633

commit v3 on v2

--- a/solution.py
+++ b/solution.py
@@ -41,6 +41,13 @@
 FULL = 32000.0
 
 
+def hops(s):
+    return sum(min(n, 4 - n) for n in (s >> 4, (s >> 2) & 3)) + ((s >> 1) & 1)
+
+
+FAR_FIRST = sorted(range(1, MEMBERS), key=lambda s: -hops(s))
+
+
 def dot(a, b, dims=NN):
     return lax.dot_general(a, b, dims, preferred_element_type=F32)
 
@@ -150,7 +157,7 @@
     ranks = jnp.where(present, rank, 0.0).T.astype(BF16)
     low_index = iota((256, BLOCK), 0)
 
-    @pl.loop(0, ROWS // BLOCK)
+    @pl.loop(0, ROWS // BLOCK, unroll=2)
     def _(b):
         span = pl.ds(pl.multiple_of(b * BLOCK, BLOCK), BLOCK)
         slot = slots[:, span]
@@ -174,7 +181,7 @@
 def describe(me, slots, places, meta, packed):
     meta[...] = jnp.zeros(meta.shape, F32)
 
-    @pl.loop(0, ROWS // BLOCK)
+    @pl.loop(0, ROWS // BLOCK, unroll=2)
     def _(b):
         span = pl.ds(pl.multiple_of(b * BLOCK, BLOCK), BLOCK)
         slot = slots[:, span]
@@ -460,18 +467,19 @@
         return pl.ds(pl.multiple_of(q * KEY_DEV, KEY_DEV), KEY_DEV)
 
     slot_total = hist[...]
-    for s in range(1, GROUPS):
+    order = (2, 1, 3)
+    for n, s in enumerate(order):
         fixed, exponents = encode(acc[part_of(lax.rem(group + s, GROUPS)), :])
         extra = jnp.concatenate(
             [slot_total, *exponents, jnp.zeros((EXTRA - OWN_ROWS - 4, LANES), F32)], axis=0
         )
         out2[s, KEY_DEV : KEY_DEV + EXTRA] = extra.astype(I32).astype(I16)
         out2[s, 0:KEY_DEV] = fixed.astype(I16)
-        if s > 1:
-            two_copy(s - 1).start()
+        if n > 0:
+            two_copy(order[n - 1]).start()
     slot = sp[part_of(group), :].astype(I32)
     totals[...] = acc[part_of(group), :]
-    two_copy(GROUPS - 1).start()
+    two_copy(order[-1]).start()
     hm_in[0] = hm_out[me]
 
     @pl.loop(1, MEMBERS)
@@ -482,7 +490,7 @@
         member_copy(s).wait_recv()
 
     heavy_total = jnp.sum(hm_in[...], axis=0)
-    for s in range(1, GROUPS):
+    for s in (1, 3, 2):
         two_copy(s).wait_recv()
         part = in2[s, KEY_DEV : KEY_DEV + EXTRA].astype(I32).astype(F32)
         slot_total = slot_total + part[0:OWN_ROWS]
@@ -510,7 +518,7 @@
         )
         sized.append(heavy_total[h : h + 1] * lax.rsqrt(1.0 + number))
 
-    for s in range(1, MEMBERS):
+    for s in FAR_FIRST:
         three_copy(s).start()
 
     @pl.when(alone)

time: 82.2 us -> 79.9 us (0.972)
  Pallas kernels: 81.3 us -> 79.1 us
    pallas_call x1, Pallas kernels: 79.8 us -> 77.5 us  [body(): pl.pallas_call(fused, out_shape=outs, in_specs=[SMEM] + [VMEM] * 2 + [ANY...]
where the time goes in v3:
time: 79.9 us; the launch traced here: 79.7 us
  Pallas kernels  79.1 us (99%)
    pallas_call x1, Pallas kernels, body(): pl.pallas_call(fused, out_shape=outs, in_specs=[SMEM] + [VMEM] * 2 + [ANY...  77.5 us

profile of v3, /device:TPU:1, one launch (start us, length us, event | category | flops | bytes accessed | tf_op | source)
XLA Modules:
  0.0 79.7 jit_solution(18429011608763517070)
XLA Ops:
  0.6 77.5 %shard_map.76 = (bf16[512,128]{1,0:T(8,128)(2,1)}, bf16[2,128]{1,0:T(2,128)(2,1)}, f32[4,128]{1,0:T(4,128)}) custom-call(s32[512]{0:T(512)} %heavy.1, s32[1,8192]{1,0:T(1,128)} %bitcast.5, s32[1,512]{1,0:T(1,128)} %bitcast.6, s32[1024,128]{1,0:T(8,128)} %bitcast.4, bf16[8192,128]{1,0:T(8,128)(2,1)} %measures_hbm.1, bf16[512,128]{1,0:T(8,128)(2,1)} %orders_hbm.1), custom_call_target="tpu_custom_call" | custom-call | tf_op jit(solution)/shard_map/pallas_call | solution.py:588
  78.1 1.6 %shard_map.77 = (bf16[512,128]{1,0:T(8,128)(2,1)}, bf16[2,128]{1,0:T(2,128)(2,1)}, f32[4,128]{1,0:T(4,128)}) custom-call(bf16[512,128]{1,0:T(8,128)(2,1)} %get-tuple-element.9.refs_0_, bf16[2,128]{1,0:T(2,128)(2,1)} %get-tuple-element.10.refs_1_, f32[4,128]{1,0:T(4,128)} %get-tuple-element.11.refs_2_), custom_call_target="tpu_custom_call" | custom-call | tf_op jit(solution)/shard_map/pallas_call | solution.py:641

commit v4 on v3

--- a/solution.py
+++ b/solution.py
@@ -219,7 +219,7 @@
     local[...] = mine_slot.astype(F32)
     eight = iota((KPP, LANES), 0).astype(F32)
 
-    @pl.loop(0, GX)
+    @pl.loop(0, GX, unroll=4)
     def _(x):
         at = pl.ds(pl.multiple_of(x * 16, 16), 16)
         ranks, locals_ = rank[at, :], local[at, :]
@@ -484,9 +484,6 @@
 
     @pl.loop(1, MEMBERS)
     def _(s):
-        main_copy(s).wait_send()
-        side_copy(s).wait_send()
-        member_copy(s).wait_send()
         member_copy(s).wait_recv()
 
     heavy_total = jnp.sum(hm_in[...], axis=0)
@@ -528,6 +525,12 @@
     @pl.when(jnp.logical_not(alone))
     def _():
         slot_copy().start()
+
+    @pl.loop(1, MEMBERS)
+    def _(s):
+        main_copy(s).wait_send()
+        side_copy(s).wait_send()
+        member_copy(s).wait_send()
 
     line = iota((KEY_DEV, LANES), 0)
     fetch_orders.wait()

time: 79.9 us -> 80.1 us (level)
  no operation moved by 1% of the time
where the time goes in v4:
time: 80.1 us; the launch traced here: 79.9 us
  Pallas kernels  79.3 us (99%)
    pallas_call x1, Pallas kernels, body(): pl.pallas_call(fused, out_shape=outs, in_specs=[SMEM] + [VMEM] * 2 + [ANY...  77.7 us

profile of v4, /device:TPU:1, one launch (start us, length us, event | category | flops | bytes accessed | tf_op | source)
XLA Modules:
  0.0 79.9 jit_solution(1517580745119133215)
XLA Ops:
  0.6 77.7 %shard_map.76 = (bf16[512,128]{1,0:T(8,128)(2,1)}, bf16[2,128]{1,0:T(2,128)(2,1)}, f32[4,128]{1,0:T(4,128)}) custom-call(s32[512]{0:T(512)} %heavy.1, s32[1,8192]{1,0:T(1,128)} %bitcast.5, s32[1,512]{1,0:T(1,128)} %bitcast.6, s32[1024,128]{1,0:T(8,128)} %bitcast.4, bf16[8192,128]{1,0:T(8,128)(2,1)} %measures_hbm.1, bf16[512,128]{1,0:T(8,128)(2,1)} %orders_hbm.1), custom_call_target="tpu_custom_call" | custom-call | tf_op jit(solution)/shard_map/pallas_call | solution.py:591
  78.4 1.6 %shard_map.77 = (bf16[512,128]{1,0:T(8,128)(2,1)}, bf16[2,128]{1,0:T(2,128)(2,1)}, f32[4,128]{1,0:T(4,128)}) custom-call(bf16[512,128]{1,0:T(8,128)(2,1)} %get-tuple-element.9.refs_0_, bf16[2,128]{1,0:T(2,128)(2,1)} %get-tuple-element.10.refs_1_, f32[4,128]{1,0:T(4,128)} %get-tuple-element.11.refs_2_), custom_call_target="tpu_custom_call" | custom-call | tf_op jit(solution)/shard_map/pallas_call | solution.py:644
